TPU v7x, 128 devices: a whole 4x4x4 slice. The times are simulated.
128 devices in a mesh: fsdp: 16 (over y_hi, z, core), tensor: 8 (over y_lo, x).
Axes of the slice: x: 4, y: 4 (y_hi: 2, y_lo: 2; y = y_hi * 2 + y_lo), z: 4, core: 2. Of those that a mesh axis runs over, the one named last changes fastest.
Arguments:
- states: bfloat16 [4096, 8192], P('fsdp'), may hold values from -64 to 64
- segment_ids: int32 [16, 256], P('fsdp'), may hold values from 0 to 3, never falling along the last dimension, each value on 1 to 128 neighbouring positions
- attn_gain: float32 [8192], replicated, may hold values from 0.1 to 1.9
- query_weight: bfloat16 [8192, 4096], P('fsdp', 'tensor'), may hold values from -2 to 2
- key_weight: bfloat16 [8192, 1024], P('fsdp', 'tensor'), may hold values from -2 to 2
- value_matrix: bfloat16 [8192, 1024], P('fsdp', 'tensor'), may hold values from -0.0625 to 0.0625
- out_weight: bfloat16 [4096, 8192], P('tensor', 'fsdp'), may hold values from -0.28125 to 0.28125
- final_gain: float32 [8192], P('tensor'), may hold values from 0.1 to 1.9
- head_weight: float32 [8192], P('tensor'), may hold values from -0.0625 to 0.0625
Outputs:
- scores: float32 [4096], P(('fsdp', 'tensor'))
- resid_out: bfloat16 [4096, 8192], P('fsdp', 'tensor')
Inputs may be any that keep to these rules, and one draw needn't show every extreme that they name: `segment_ids`: in each row, segment numbers never fall and each rollout spans 1 to 128 positions.
All inputs are finite; a program needn't handle non-finite values.
Results may differ from a plain program's by a relative error of at most 0.0071.
Values may be sent and summed in bfloat16 or wider, within the bound.
A program may use at most 128 MiB of HBM per device.

v0:
```python
import jax
import jax.numpy as jnp
from jax import lax
from jax.sharding import PartitionSpec as P

MODEL_WIDTH = 8192
HEAD_SIZE = 128
EPS = 1e-05
THETA = 500000.0
NEG_FILL = -1e30


def in_one_piece(arrays, axis, dim, along):
    both = jnp.concatenate(arrays, axis=along)
    result, at, outs = (lax.all_gather(both, axis, axis=dim, tiled=True), 0, [])
    for a in arrays:
        outs.append(lax.slice_in_dim(result, at, at + a.shape[along], axis=along))
        at += a.shape[along]
    return tuple(outs)


def sent_to_all(value, axis):
    length = lax.axis_size(axis)
    return lax.all_to_all(
        jnp.broadcast_to(value[None], (length, *value.shape)), axis, 0, 0, tiled=True
    )


def over_copies(value, axis):
    return sent_to_all(value, axis).sum(axis=0)


def together(arrays, axis):
    ravelled, at, outs = (jnp.concatenate([a.reshape(-1) for a in arrays]), 0, [])
    total = over_copies(ravelled, axis)
    for a in arrays:
        outs.append(total[at : at + a.size].reshape(a.shape))
        at += a.size
    return tuple(outs)


def rope_tables(seg_row):
    count = seg_row.shape[0]
    places = jnp.arange(count, dtype=jnp.int32)
    boundary = jnp.concatenate([jnp.ones((1,), dtype=bool), seg_row[1:] != seg_row[:-1]])
    begins = lax.cummax(jnp.where(boundary, places, jnp.zeros_like(places)), axis=0)
    positions = (places - begins).astype(jnp.float32)
    half_width = HEAD_SIZE // 2
    frequency = THETA ** (-(2.0 * jnp.arange(half_width, dtype=jnp.float32)) / HEAD_SIZE)
    angles = positions[:, None] * frequency[None, :]
    return (jnp.cos(angles), jnp.sin(angles))


def rotated(block, cosine, sine_part):
    half_width = block.shape[-1] // 2
    first_half = block[..., :half_width]
    second_half = block[..., half_width:]
    cos_rows = cosine[:, None, :]
    sin_rows = sine_part[:, None, :]
    return jnp.concatenate(
        [
            first_half * cos_rows - second_half * sin_rows,
            second_half * cos_rows + first_half * sin_rows,
        ],
        axis=-1,
    )


def attend(queries, key_rows, values, seg_row):
    t_rows = queries.shape[0]
    heads_here = queries.shape[1] // HEAD_SIZE
    groups_here = key_rows.shape[1] // HEAD_SIZE
    ratio = heads_here // groups_here
    cosine, sine_part = rope_tables(seg_row)
    query_rot = rotated(queries.reshape(t_rows, heads_here, HEAD_SIZE), cosine, sine_part).astype(
        jnp.bfloat16
    )
    key_rot = rotated(key_rows.reshape(t_rows, groups_here, HEAD_SIZE), cosine, sine_part).astype(
        jnp.bfloat16
    )
    value_rows = values.astype(jnp.bfloat16).reshape(t_rows, groups_here, HEAD_SIZE)
    grouped = query_rot.reshape(t_rows, groups_here, ratio, HEAD_SIZE)
    logits = jnp.einsum(
        "tkgd,skd->kgts", grouped, key_rot, preferred_element_type=jnp.float32
    ) * HEAD_SIZE ** (-0.5)
    places = jnp.arange(t_rows, dtype=jnp.int32)
    allowed = (seg_row[:, None] == seg_row[None, :]) & (places[None, :] <= places[:, None])
    logits = jnp.where(allowed[None, None], logits, NEG_FILL)
    row_peak = jnp.max(logits, axis=-1, keepdims=True)
    raised = jnp.exp(logits - row_peak)
    probabilities = (raised / jnp.sum(raised, axis=-1, keepdims=True)).astype(jnp.bfloat16)
    mixed = jnp.einsum(
        "kgts,skd->tkgd", probabilities, value_rows, preferred_element_type=jnp.float32
    )
    return mixed.astype(jnp.bfloat16).reshape(t_rows, heads_here * HEAD_SIZE)


def body(
    states,
    segment_ids,
    attn_gain,
    query_weight,
    key_weight,
    value_matrix,
    out_weight,
    final_gain,
    head_weight,
):
    t_rows, width = states.shape
    tensor_count = lax.axis_size("tensor")
    tensor_index = lax.axis_index("tensor")
    widened = states.astype(jnp.float32)
    normed = (
        widened
        * lax.rsqrt(jnp.sum(widened * widened, axis=1, keepdims=True) / MODEL_WIDTH + EPS)
        * attn_gain[None, :]
    ).astype(jnp.bfloat16)

    def add_piece(portion):
        return jnp.dot(normed, portion, preferred_element_type=jnp.float32)

    pieces = in_one_piece((query_weight, key_weight, value_matrix), "fsdp", 0, 1)
    queries = add_piece(pieces[0])
    key_rows = add_piece(pieces[1])
    values = add_piece(pieces[2])
    mixed = attend(queries, key_rows, values, segment_ids[0])
    slice_cols = width // tensor_count
    partials = jnp.dot(
        mixed,
        lax.all_gather(out_weight, "fsdp", axis=1, tiled=True),
        preferred_element_type=jnp.float32,
    )
    branch = lax.psum_scatter(partials, "tensor", scatter_dimension=1, tiled=True)
    own_cols = lax.dynamic_slice_in_dim(widened, tensor_index * slice_cols, slice_cols, 1)
    resid_out = (own_cols + branch).astype(jnp.bfloat16)
    stream = resid_out.astype(jnp.float32)
    squares = jnp.sum(stream * stream, axis=1)
    products = jnp.sum(stream * (final_gain * head_weight)[None, :], axis=1)
    share_rows = t_rows // tensor_count
    squares_all, products_all = together((squares, products), "tensor")
    local_squares = lax.dynamic_slice_in_dim(squares_all, tensor_index * share_rows, share_rows, 0)
    products_mine = lax.dynamic_slice_in_dim(products_all, tensor_index * share_rows, share_rows, 0)
    scores = products_mine * lax.rsqrt(local_squares / MODEL_WIDTH + EPS)
    return (scores, resid_out)


def solution(mesh):
    placed = (
        P("fsdp", None),
        P("fsdp", None),
        P(),
        P("fsdp", "tensor"),
        P("fsdp", "tensor"),
        P("fsdp", "tensor"),
        P("tensor", "fsdp"),
        P("tensor"),
        P("tensor"),
    )
    return jax.shard_map(
        body,
        mesh=mesh,
        in_specs=placed,
        out_specs=(P(("fsdp", "tensor")), P("fsdp", "tensor")),
        check_vma=False,
    )
```

profile of v0, /device:TPU:0, one launch (start us, length us, event | category | flops | bytes accessed | tf_op | source)
XLA Modules:
  0.0 299.0 jit_solution(9830881361931489665)
XLA Ops:
  7.2 0.0 all-gather.3.cloned.1.call-start
  7.2 2.1 pad_maximum_fusion
  9.3 0.0 all-gather.3.cloned.1.call-update
  9.4 0.0 all-gather.5.cloned.1.call-start
  9.4 0.7 all-gather.5.cloned.1.call-update
  10.1 0.0 reduce-scatter.2.cloned.1.call-start
  10.2 0.8 compare_reduce_fusion
  11.0 0.1 fusion.40
  11.1 0.3 reduce-window.9
  11.4 0.1 slice.47
  11.5 0.1 slice_reduce_fusion
  11.6 3.1 %multiply_reduce_fusion = f32[256]{0:T(256)S(1)} fusion(bf16[256,8192]{1,0:T(8,128)(2,1)} %param.9), kind=kLoop, calls=%fused_computation.3 | loop fusion | flops 6291200 | bytes 4195328 | tf_op jit(solution)/shard_map/reduce_sum | solution.py:115
  14.8 0.1 fusion.41
  14.8 0.9 fusion.27
  15.7 0.5 multiply_cosine_fusion
  16.2 0.0 copy-start.2
  16.2 87.3 %all-gather.3.cloned.1.call-done = bf16[8192,768]{1,0:T(8,128)(2,1)} async-done(((bf16[512,768]{1,0:T(8,128)(2,1)}), bf16[8192,768]{1,0:T(8,128)(2,1)}) %all-gather.3.cloned.1.call-update) | async-done | bytes 12582928 | tf_op jit(solution)/shard_map/all_gather | solution.py:15
  103.6 7.1 %fusion = f32[256,512]{1,0:T(8,128)S(1)} fusion(bf16[8192,768]{1,0:T(8,128)(2,1)} %all-gather.3.cloned.1.call-done, f32[8192]{0:T(1024)} %param.11, f32[256]{0:T(256)S(1)} %add_rsqrt_fusion, bf16[256,8192]{1,0:T(8,128)(2,1)} %param.9), kind=kOutput, calls=%fused_computation | convolution fusion | flops 2155872256 | bytes 13140992 | tf_op jit(solution)/shard_map/dot_general | solution.py:120
  110.6 0.2 reshape.251
  110.8 0.0 copy-done.2
  110.8 4.9 %fusion.8 = f32[256,1,128]{0,2,1:T(8,128)S(1)} fusion(bf16[8192,768]{1,0:T(8,128)(2,1)} %all-gather.3.cloned.1.call-done, f32[8192]{0:T(1024)S(1)} %copy-done.2, f32[256]{0:T(256)S(1)} %add_rsqrt_fusion, bf16[256,8192]{1,0:T(8,128)(2,1)} %param.9), kind=kOutput, calls=%fused_computation.14 | convolution fusion | flops 545259520 | bytes 6456320 | tf_op jit(solution)/shard_map/dot_general | solution.py:120
  115.7 0.3 fusion.39
  116.0 0.3 fusion.43
  116.4 0.1 subtract_convert_fusion
  116.5 0.4 fusion.45
  117.0 0.2 fusion.21
  117.1 4.6 %convolution_convert_fusion = bf16[128,4,256]{2,0,1:T(8,128)(2,1)S(1)} fusion(bf16[8192,768]{1,0:T(8,128)(2,1)} %all-gather.3.cloned.1.call-done, f32[1,4,256,256]{2,3,1,0:T(8,128)S(1)} %get-tuple-element.16, f32[4,256]{1,0:T(4,128)S(1)} %fusion.21, f32[4,256]{1,0:T(4,128)S(1)} %get-tuple-element.15, f32[8192]{0:T(1024)S(1)} %copy-done.2, ...), kind=kOutput, calls=%fused_computation.13 | convolution fusion | flops 613318656 | bytes 7644160 | tf_op jit(solution)/shard_map/kgts,skd->tkgd/dot_general | solution.py:92
  121.7 58.3 %all-gather.5.cloned.1.call-done = bf16[512,8192]{1,0:T(8,128)(2,1)} async-done(((bf16[512,512]{1,0:T(8,128)(2,1)}), bf16[512,8192]{1,0:T(8,128)(2,1)}) %all-gather.5.cloned.1.call-update) | async-done | bytes 8388624 | tf_op jit(solution)/shard_map/all_gather | solution.py:130
  180.0 9.0 %fusion.46 = f32[256,8192]{1,0:T(8,128)} fusion(bf16[256,512]{0,1:T(8,128)(2,1)S(1)} %bitcast.40, bf16[512,8192]{1,0:T(8,128)(2,1)} %all-gather.5.cloned.1.call-done), kind=kOutput, calls=%fused_computation.64 | convolution fusion | flops 2147483648 | bytes 17039360 | tf_op jit(solution)/shard_map/dot_general | solution.py:128
  189.0 0.0 reduce-scatter.2.cloned.1.call-update
  189.0 0.0 copy-start
  189.1 0.0 copy-start.1
  189.1 6.7 %convert_element_type.41 = f32[256,8192]{1,0:T(8,128)} convert(bf16[256,8192]{1,0:T(8,128)(2,1)} %param.9) | non-fusion elementwise | flops 2097152 | bytes 12582912 | tf_op jit(solution)/shard_map/convert_element_type | solution.py:112
  195.7 0.0 copy-done
  195.7 0.0 copy-done.1
  195.7 83.5 %reduce-scatter.2.cloned.1.call-done = f32[256,1024]{1,0:T(8,128)} async-done(((f32[256,8192]{1,0:T(8,128)}), f32[256,1024]{1,0:T(8,128)}) %reduce-scatter.2.cloned.1.call-update) | async-done | bytes 1048592 | tf_op jit(solution)/shard_map/reduce_scatter | solution.py:133
  279.2 2.5 fusion.19
  281.8 0.6 broadcast_in_dim.15
  282.4 3.3 %all-to-all-start = ((f32[8,1,512]{2,1,0:T(1,128)}), f32[8,1,512]{2,1,0:T(1,128)S(1)}, u32[]{:S(2)}, u32[]{:S(2)}) async-start(f32[8,1,512]{2,1,0:T(1,128)} %broadcast_in_dim.15), calls=%async_computation.1 | async-start | bytes 32768 | tf_op jit(solution)/shard_map/all_to_all | solution.py:24
  285.7 6.1 %all-to-all-done = f32[8,1,512]{2,1,0:T(1,128)S(1)} async-done(((f32[8,1,512]{2,1,0:T(1,128)}), f32[8,1,512]{2,1,0:T(1,128)S(1)}, u32[]{:S(2)}, u32[]{:S(2)}) %all-to-all-start) | async-done | bytes 16416 | tf_op jit(solution)/shard_map/all_to_all | solution.py:24
  291.9 0.6 rsqrt_multiply_fusion
  (7 shorter events, 0.1 us)
Async XLA Ops:
  7.2 96.4 %all-gather.3.cloned.1.call-start = ((), (), s32[]{:S(2)}) async-start(), calls=%async_computation.2 | async-start | bytes 13369344 | tf_op jit(solution)/shard_map/all_gather | solution.py:15
  9.4 170.7 %all-gather.5.cloned.1.call-start = ((), (), s32[]{:S(2)}) async-start(), calls=%async_computation.3 | async-start | bytes 8912896 | tf_op jit(solution)/shard_map/all_gather | solution.py:130
  10.1 269.1 %reduce-scatter.2.cloned.1.call-start = ((), (), s32[]{:S(2)}) async-start(), calls=%async_computation.4 | async-start | bytes 9437184 | tf_op jit(solution)/shard_map/reduce_scatter | solution.py:133
  16.2 94.6 %copy-start.2 = (f32[8192]{0:T(1024)S(1)}, f32[8192]{0:T(1024)}, u32[]{:S(2)}) copy-start(f32[8192]{0:T(1024)} %param.11) | copy-start | bytes 98308
  189.0 6.7 %copy-start = (f32[1024]{0:T(1024)S(1)}, f32[1024]{0:T(1024)}, u32[]{:S(2)}) copy-start(f32[1024]{0:T(1024)} %param.16) | copy-start | bytes 12292
  189.1 6.7 %copy-start.1 = (f32[1024]{0:T(1024)S(1)}, f32[1024]{0:T(1024)}, u32[]{:S(2)}) copy-start(f32[1024]{0:T(1024)} %param.17) | copy-start | bytes 12292
  282.4 9.5 %all-to-all-start = ((f32[8,1,512]{2,1,0:T(1,128)}), f32[8,1,512]{2,1,0:T(1,128)S(1)}, u32[]{:S(2)}, u32[]{:S(2)}) async-start(f32[8,1,512]{2,1,0:T(1,128)} %broadcast_in_dim.15), calls=%async_computation.1 | async-start | bytes 32768 | tf_op jit(solution)/shard_map/all_to_all | solution.py:24
Sparse Core Ops, SparseCore 0:
  10.5 93.0 all-gather.2
  105.8 74.1 all-gather.4
  189.2 90.0 reduce-scatter.1
where the time goes:
time: 299 us
  waiting for transfers between devices  236 us (79%)
  matrix products  25.9 us (9%)
  other arithmetic  18.4 us (6%)
  between operations  13.9 us (5%)
  starting transfers between devices  3.45 us (1%)
    all_gather x1, waiting for transfers between devices, in_one_piece(): result, at, outs = (lax.all_gather(both, axis, axis=dim, tiled=True), 0, [])  87.3 us
    reduce_scatter x1, waiting for transfers between devices, body(): lax.psum_scatter(partials, 'tensor', scatter_dimension=1, tiled=True)  83.5 us
    all_gather x1, waiting for transfers between devices, body(): lax.all_gather(out_weight, 'fsdp', axis=1, tiled=True)  58.3 us
    dot_general x2, matrix products, add_piece(): return jnp.dot(normed, portion, preferred_element_type=jnp.float32)  11.9 us
    dot_general x1, matrix products, body(): jnp.dot(mixed, lax.all_gather(out_weight, 'fsdp', axis=1, tiled=True), pr...  8.98 us
    convert_element_type x1, other arithmetic, body(): widened = states.astype(jnp.float32)  6.65 us
    all_to_all x1, waiting for transfers between devices, sent_to_all(): lax.all_to_all(jnp.broadcast_to(value[None], (length, *value.shape)), axi...  6.14 us
  transfers between devices with their start and end apart: 4, of which 4 were waited for; matrix products, arithmetic and copies ran while one was open for 10% of the time, Pallas kernels for 0%

commit v1 on v0

--- a/solution.py
+++ b/solution.py
@@ -106,6 +106,13 @@
     final_gain,
     head_weight,
 ):
+
+    def draw_pipes(matrix):
+        formed = tuple((matrix for _ in range(lax.psum(1, axis_name="fsdp"))))
+        then = jnp.stack(formed)
+        newest = lax.all_to_all(then, concat_axis=0, axis_name="fsdp", split_axis=0)
+        return jnp.concatenate(newest, 1)
+
     t_rows, width = states.shape
     tensor_count = lax.axis_size("tensor")
     tensor_index = lax.axis_index("tensor")
@@ -125,11 +132,7 @@
     values = add_piece(pieces[2])
     mixed = attend(queries, key_rows, values, segment_ids[0])
     slice_cols = width // tensor_count
-    partials = jnp.dot(
-        mixed,
-        lax.all_gather(out_weight, "fsdp", axis=1, tiled=True),
-        preferred_element_type=jnp.float32,
-    )
+    partials = jnp.dot(mixed, draw_pipes(out_weight), preferred_element_type=jnp.float32)
     branch = lax.psum_scatter(partials, "tensor", scatter_dimension=1, tiled=True)
     own_cols = lax.dynamic_slice_in_dim(widened, tensor_index * slice_cols, slice_cols, 1)
     resid_out = (own_cols + branch).astype(jnp.bfloat16)

time: 299 us -> 336 us (1.12)
  waiting for transfers between devices: 236 us -> 260 us
  starting transfers between devices: 3.45 us -> 11.8 us
  local copies, waits for them, and re-layouts: 1.34 us -> 6.69 us
    all_gather x1, waiting for transfers between devices: 87.3 us -> 168 us  [in_one_piece(): result, at, outs = (lax.all_gather(both, axis, axis=dim, tiled=True), 0, [])]
    all_gather x1 -> x0, waiting for transfers between devices: 58.3 us -> none  [body(): lax.all_gather(out_weight, 'fsdp', axis=1, tiled=True)]
    all_to_all x0 -> x1, starting transfers between devices: none -> 8.34 us  [draw_pipes(): newest = lax.all_to_all(then, concat_axis=0, axis_name='fsdp', split_axis=0)]
    another operation x1 -> x2, local copies, waits for them, and re-layouts: 0.11 us -> 4.21 us  [the longest x1 4.09 us: draw_pipes(): then = jnp.stack(formed)]
  transfers between devices with their start and end apart: 4 -> 4, of which waited for: 4 -> 3; matrix products, arithmetic and copies ran while one was open for 10% -> 10% of each run, Pallas kernels for 0% -> 0%
where the time goes in v1:
time: 336 us; the launch traced here: 335 us
  waiting for transfers between devices  260 us (77%)
  matrix products  25.7 us (8%)
  other arithmetic  16.9 us (5%)
  between operations  14.2 us (4%)
  starting transfers between devices  11.8 us (4%)
  local copies, waits for them, and re-layouts  6.69 us (2%)
    all_gather x1, waiting for transfers between devices, in_one_piece(): result, at, outs = (lax.all_gather(both, axis, axis=dim, tiled=True), 0, [])  168 us
    reduce_scatter x1, waiting for transfers between devices, body(): lax.psum_scatter(partials, 'tensor', scatter_dimension=1, tiled=True)  86.4 us
    dot_general x2, matrix products, add_piece(): return jnp.dot(normed, portion, preferred_element_type=jnp.float32)  11.7 us
    dot_general x1, matrix products, body(): jnp.dot(mixed, draw_pipes(out_weight), preferred_element_type=jnp.float32)  9.02 us
    all_to_all x1, starting transfers between devices, draw_pipes(): newest = lax.all_to_all(then, concat_axis=0, axis_name='fsdp', split_axis=0)  8.34 us
  transfers between devices with their start and end apart: 4, of which 3 were waited for; matrix products, arithmetic and copies ran while one was open for 10% of the time, Pallas kernels for 0%

profile of v1, /device:TPU:0, one launch (start us, length us, event | category | flops | bytes accessed | tf_op | source)
XLA Modules:
  0.0 335.3 jit_solution(15507325769160504709)
XLA Ops:
  7.2 0.0 all-gather.2.cloned.1.call-start
  7.2 2.2 pad_maximum_fusion
  9.4 0.0 all-gather.2.cloned.1.call-update
  9.4 1.3 copy.31
  10.7 4.1 %stack.2 = bf16[16,512,512]{1,2,0:T(8,128)(2,1)} broadcast(bf16[512,512]{0,1:T(8,128)(2,1)S(1)} %copy.31), dimensions={1,2} | broadcast | bytes 8912896 | tf_op jit(solution)/shard_map/stack | solution.py:112
  14.7 0.0 copy-start
  14.8 0.0 copy-start.3
  14.8 8.3 %all-to-all-start = ((bf16[16,512,512]{1,2,0:T(8,128)(2,1)}), bf16[16,512,512]{1,2,0:T(8,128)(2,1)}, u32[]{:S(2)}, u32[]{:S(2)}) async-start(bf16[16,512,512]{1,2,0:T(8,128)(2,1)} %stack.2), calls=%async_computation | async-start | bytes 16777216 | tf_op jit(solution)/shard_map/all_to_all | solution.py:113
  23.1 0.0 reduce-scatter.2.cloned.1.call-start
  23.2 0.0 copy-done
  23.2 0.1 compare_reduce_fusion
  23.3 0.1 fusion.40
  23.3 0.3 reduce-window.9
  23.6 0.1 slice.47
  23.8 0.1 slice_reduce_fusion
  23.9 3.3 multiply_reduce_fusion
  27.2 0.1 fusion.41
  27.3 0.1 fusion.27
  27.4 0.5 multiply_cosine_fusion
  28.0 167.5 %all-gather.2.cloned.1.call-done = bf16[8192,768]{1,0:T(8,128)(2,1)} async-done(((bf16[512,768]{1,0:T(8,128)(2,1)}), bf16[8192,768]{1,0:T(8,128)(2,1)}) %all-gather.2.cloned.1.call-update) | async-done | bytes 12582928 | tf_op jit(solution)/shard_map/all_gather | solution.py:15
  195.5 0.0 copy-done.3
  195.5 7.0 %fusion = f32[256,512]{1,0:T(8,128)S(1)} fusion(bf16[8192,768]{1,0:T(8,128)(2,1)} %all-gather.2.cloned.1.call-done, f32[8192]{0:T(1024)S(1)} %copy-done.3, f32[256]{0:T(256)S(1)} %add_rsqrt_fusion, bf16[256,8192]{1,0:T(8,128)(2,1)} %param.9), kind=kOutput, calls=%fused_computation | convolution fusion | flops 2155872256 | bytes 13140992 | tf_op jit(solution)/shard_map/dot_general | solution.py:127
  202.5 0.2 reshape.259
  202.7 4.6 %fusion.8 = f32[256,1,128]{0,2,1:T(8,128)S(1)} fusion(bf16[8192,768]{1,0:T(8,128)(2,1)} %all-gather.2.cloned.1.call-done, f32[8192]{0:T(1024)S(1)} %copy-done.3, f32[256]{0:T(256)S(1)} %add_rsqrt_fusion, bf16[256,8192]{1,0:T(8,128)(2,1)} %param.9), kind=kOutput, calls=%fused_computation.14 | convolution fusion | flops 545259520 | bytes 6456320 | tf_op jit(solution)/shard_map/dot_general | solution.py:127
  207.3 0.3 fusion.39
  207.6 0.3 fusion.43
  208.0 0.1 subtract_convert_fusion
  208.1 0.4 fusion.45
  208.6 0.2 fusion.21
  208.7 4.6 %convolution_convert_fusion = bf16[128,4,256]{2,0,1:T(8,128)(2,1)S(1)} fusion(bf16[8192,768]{1,0:T(8,128)(2,1)} %all-gather.2.cloned.1.call-done, f32[1,4,256,256]{2,3,1,0:T(8,128)S(1)} %get-tuple-element.16, f32[4,256]{1,0:T(4,128)S(1)} %fusion.21, f32[4,256]{1,0:T(4,128)S(1)} %get-tuple-element.15, f32[8192]{0:T(1024)S(1)} %copy-done.3, ...), kind=kOutput, calls=%fused_computation.13 | convolution fusion | flops 613318656 | bytes 7644160 | tf_op jit(solution)/shard_map/kgts,skd->tkgd/dot_general | solution.py:92
  213.3 0.0 all-to-all-done
  213.3 9.0 %fusion.46 = f32[256,8192]{1,0:T(8,128)} fusion(bf16[256,512]{0,1:T(8,128)(2,1)S(1)} %bitcast.43, bf16[512,8192]{0,1:T(8,128)(2,1)} %bitcast.15), kind=kOutput, calls=%fused_computation.64 | convolution fusion | flops 2147483648 | bytes 17039360 | tf_op jit(solution)/shard_map/dot_general | solution.py:135
  222.3 0.0 reduce-scatter.2.cloned.1.call-update
  222.4 0.0 copy-start.1
  222.4 0.0 copy-start.2
  222.4 6.4 %convert_element_type.41 = f32[256,8192]{1,0:T(8,128)} convert(bf16[256,8192]{1,0:T(8,128)(2,1)} %param.9) | non-fusion elementwise | flops 2097152 | bytes 12582912 | tf_op jit(solution)/shard_map/convert_element_type | solution.py:119
  228.8 0.0 copy-done.1
  228.8 0.0 copy-done.2
  228.8 86.4 %reduce-scatter.2.cloned.1.call-done = f32[256,1024]{1,0:T(8,128)} async-done(((f32[256,8192]{1,0:T(8,128)}), f32[256,1024]{1,0:T(8,128)}) %reduce-scatter.2.cloned.1.call-update) | async-done | bytes 1048592 | tf_op jit(solution)/shard_map/reduce_scatter | solution.py:136
  315.2 2.5 fusion.19
  317.8 0.6 broadcast_in_dim.15
  318.4 3.3 all-to-all-start.1
  321.7 6.1 %all-to-all-done.1 = f32[8,1,512]{2,1,0:T(1,128)S(1)} async-done(((f32[8,1,512]{2,1,0:T(1,128)}), f32[8,1,512]{2,1,0:T(1,128)S(1)}, u32[]{:S(2)}, u32[]{:S(2)}) %all-to-all-start.1) | async-done | bytes 16416 | tf_op jit(solution)/shard_map/all_to_all | solution.py:24
  327.9 0.6 rsqrt_multiply_fusion
  (7 shorter events, 0.1 us)
Async XLA Ops:
  7.2 188.3 %all-gather.2.cloned.1.call-start = ((), (), s32[]{:S(2)}) async-start(), calls=%async_computation.3 | async-start | bytes 13369344 | tf_op jit(solution)/shard_map/all_gather | solution.py:15
  14.7 8.4 %copy-start = (s32[1,256]{1,0:T(1,128)S(1)}, s32[1,256]{1,0:T(1,128)}, u32[]{:S(2)}) copy-start(s32[1,256]{1,0:T(1,128)} %param.10) | copy-start | bytes 3076
  14.8 180.7 %copy-start.3 = (f32[8192]{0:T(1024)S(1)}, f32[8192]{0:T(1024)}, u32[]{:S(2)}) copy-start(f32[8192]{0:T(1024)} %param.11) | copy-start | bytes 98308
  14.8 198.6 %all-to-all-start = ((bf16[16,512,512]{1,2,0:T(8,128)(2,1)}), bf16[16,512,512]{1,2,0:T(8,128)(2,1)}, u32[]{:S(2)}, u32[]{:S(2)}) async-start(bf16[16,512,512]{1,2,0:T(8,128)(2,1)} %stack.2), calls=%async_computation | async-start | bytes 16777216 | tf_op jit(solution)/shard_map/all_to_all | solution.py:113
  23.1 292.1 %reduce-scatter.2.cloned.1.call-start = ((), (), s32[]{:S(2)}) async-start(), calls=%async_computation.4 | async-start | bytes 9437184 | tf_op jit(solution)/shard_map/reduce_scatter | solution.py:136
  222.4 6.4 %copy-start.1 = (f32[1024]{0:T(1024)S(1)}, f32[1024]{0:T(1024)}, u32[]{:S(2)}) copy-start(f32[1024]{0:T(1024)} %param.16) | copy-start | bytes 12292
  222.4 6.4 %copy-start.2 = (f32[1024]{0:T(1024)S(1)}, f32[1024]{0:T(1024)}, u32[]{:S(2)}) copy-start(f32[1024]{0:T(1024)} %param.17) | copy-start | bytes 12292
  318.4 9.5 %all-to-all-start.1 = ((f32[8,1,512]{2,1,0:T(1,128)}), f32[8,1,512]{2,1,0:T(1,128)S(1)}, u32[]{:S(2)}, u32[]{:S(2)}) async-start(f32[8,1,512]{2,1,0:T(1,128)} %broadcast_in_dim.15), calls=%async_computation.2 | async-start | bytes 32768 | tf_op jit(solution)/shard_map/all_to_all | solution.py:24
Sparse Core Ops, SparseCore 0:
  10.5 184.9 all-gather.1
  222.5 92.7 reduce-scatter.1
